TPU v7x, 32 devices: a whole 2x2x4 slice. The times are simulated.
32 devices in a mesh: grp: 4 (over y, x), shard: 8 (over z, core).
Axes of the slice: x: 2, y: 2, z: 4, core: 2. Of those that a mesh axis runs over, the one named last changes fastest.
Arguments:
- bottom_out: bfloat16 [4096, 128], P(('grp', 'shard')), may hold values from -6 to 6
- lookups: int32 [4096, 1, 4], P(('grp', 'shard')), may hold values from 0 to 62975, as said below
- starts: int32 [4, 32], replicated, may hold values from 0 to 1967
- tables: float32 [1, 62976, 128], P(None, 'shard'), may hold values from -0.3 to 0.3
- top_dense: bfloat16 [128, 1024], replicated, may hold values from -0.5 to 0.5
- top_pairs: float32 [1, 1024], replicated, may hold values from -6 to 6
- cotangent: float32 [4096, 1024], P(('grp', 'shard')), may hold values from -1.5 to 1.5
Outputs:
- activation: bfloat16 [4096, 1024], P(('grp', 'shard'))
- bottom_grad: float32 [4096, 128], P(('grp', 'shard'))
- table_grad: float32 [1, 8, 7872, 128], P(None, 'shard', 'grp')
Inputs may be any that keep to these rules, and one draw needn't show every extreme that they name: lookups % 1968 is below 64, and 63 occurs.
All inputs are finite; a program needn't handle non-finite values.
Results may differ from a plain program's by a relative error of at most 0.0023.
Values sent between devices are 32-bit elements; how exact they have to be, the bound alone decides.
A program may use at most 64 MiB of HBM per device.

v0:
```python
import math

import jax
import jax.numpy as jnp
from jax import lax
from jax.sharding import PartitionSpec as P

HOT = 64


def pair_list(number):
    return [(former, latter) for former in range(number) for latter in range(former + 1, number)]


def pool_lookups(tables, picked, offset):
    rows_count = picked.shape[0]
    table_count = picked.shape[1]
    bag_count = picked.shape[2]
    rows_block = math.gcd(rows_count, 512)
    bag_block = math.gcd(bag_count, 8)
    bag_turns = bag_count // bag_block
    span_rows = tables.shape[1]
    table_ids = jnp.arange(table_count, dtype=jnp.int32)[None, :, None]

    def pool_step(turn, running):
        row_turn = turn // bag_turns
        bag_turn = turn % bag_turns
        chosen = lax.dynamic_slice(
            picked,
            (row_turn * rows_block, 0, bag_turn * bag_block),
            (rows_block, table_count, bag_block),
        )
        local = chosen - offset
        inside = (local >= 0) & (local < span_rows)
        fetched = tables[table_ids, jnp.clip(local, 0, span_rows - 1)]
        summed = jnp.sum(jnp.where(inside[..., None], fetched, 0.0), axis=2)
        current = lax.dynamic_slice_in_dim(running, row_turn * rows_block, rows_block, 0)
        return lax.dynamic_update_slice_in_dim(running, current + summed, row_turn * rows_block, 0)

    start_value = jnp.zeros((rows_count, table_count, tables.shape[2]), jnp.float32)
    return lax.fori_loop(0, rows_count // rows_block * bag_turns, pool_step, start_value)


def add_lookups(running_grad, grads, picked, offset, span_rows):
    rows_count = picked.shape[0]
    table_count = picked.shape[1]
    bag_count = picked.shape[2]
    rows_block = math.gcd(rows_count, 512)
    bag_block = math.gcd(bag_count, 8)
    bag_turns = bag_count // bag_block
    table_ids = jnp.arange(table_count, dtype=jnp.int32)[None, :, None]

    def add_step(turn, running):
        row_turn = turn // bag_turns
        bag_turn = turn % bag_turns
        chosen = lax.dynamic_slice(
            picked,
            (row_turn * rows_block, 0, bag_turn * bag_block),
            (rows_block, table_count, bag_block),
        )
        grads_block = lax.dynamic_slice_in_dim(grads, row_turn * rows_block, rows_block, 0)
        local = chosen - offset
        inside = (local >= 0) & (local < span_rows)
        updates = jnp.where(inside[..., None], grads_block[:, :, None, :], 0.0)
        return running.at[table_ids, jnp.clip(local, 0, span_rows - 1)].add(updates)

    return lax.fori_loop(0, rows_count // rows_block * bag_turns, add_step, running_grad)


def on_device(bottom_out, lookups, starts, tables, top_dense, top_pairs, cotangent):
    shard_pos = lax.axis_index("shard")
    grp_pos = lax.axis_index("grp")
    group_count = lax.axis_size("grp")
    span_rows = tables.shape[1]
    table_count = tables.shape[0]
    width = tables.shape[2]
    win_size = span_rows // group_count
    offset = shard_pos * span_rows
    my_starts = lax.dynamic_index_in_dim(starts, grp_pos, 0, keepdims=False)
    window = lookups // win_size
    inner = lookups % win_size
    own_rows = window * win_size + (inner + my_starts[window]) % win_size
    group_idx = lax.all_gather(own_rows, "shard", axis=0, tiled=True)
    picked = group_idx
    pooled = lax.psum_scatter(
        pool_lookups(tables, picked, offset), "shard", scatter_dimension=0, tiled=True
    )
    vectors = [bottom_out.astype(jnp.float32)] + [pooled[:, 0]]
    couples = pair_list(table_count + 1)
    pair_dots = jnp.stack(
        [jnp.sum(vectors[former] * vectors[latter], axis=-1) for former, latter in couples], axis=1
    )
    preact = jnp.dot(bottom_out, top_dense, preferred_element_type=jnp.float32)
    preact = preact + jnp.dot(pair_dots, top_pairs, precision=lax.Precision.HIGHEST)
    sigmoid_pre = jax.nn.sigmoid(preact)
    activation = (preact * sigmoid_pre).astype(jnp.bfloat16)
    pre_grad = cotangent * sigmoid_pre * (1.0 + preact * (1.0 - sigmoid_pre))
    pair_grad = jnp.dot(pre_grad, top_pairs.T, precision=lax.Precision.HIGHEST)
    vec_grads = [jnp.zeros_like(vector) for vector in vectors]
    for place, (former, latter) in enumerate(couples):
        vec_grads[former] = pair_grad * vectors[latter]
        vec_grads[latter] = pair_grad * vectors[former]
    pre_half = pre_grad.astype(jnp.bfloat16)
    bottom_grad = (
        lax.dot_general(
            pre_half, top_dense, (((1,), (1,)), ((), ())), preferred_element_type=jnp.float32
        )
        + vec_grads[0]
    )
    pooled_grad = jnp.stack(vec_grads[1:], axis=1)
    start_grad = jnp.zeros((table_count, span_rows, width), jnp.float32)
    picked = group_idx
    local_grad = add_lookups(
        start_grad,
        lax.all_gather(pooled_grad, "shard", axis=0, tiled=True),
        picked,
        offset,
        span_rows,
    )
    hot_range = jnp.arange(HOT, dtype=jnp.int32)
    owner_range = jnp.arange(group_count, dtype=jnp.int32)
    send_starts = lax.dynamic_slice_in_dim(my_starts, shard_pos * group_count, group_count, 0)
    send_index = (
        owner_range[:, None] * win_size + (send_starts[:, None] + hot_range[None, :]) % win_size
    )
    packed = local_grad[:, send_index]
    received = lax.all_to_all(packed, "grp", split_axis=1, concat_axis=1, tiled=True)
    recv_starts = lax.dynamic_slice_in_dim(starts, shard_pos * group_count + grp_pos, 1, 1)[:, 0]
    places = ((recv_starts[:, None] + hot_range[None, :]) % win_size).reshape(-1)
    flat_rows = received.reshape(table_count, group_count * HOT, width)
    table_grad = jnp.zeros((table_count, win_size, width), jnp.float32).at[:, places].add(flat_rows)
    return (activation, bottom_grad, table_grad[:, None])


def solution(mesh):
    in_specs = (
        P(("grp", "shard"), None),
        P(("grp", "shard"), None, None),
        P(),
        P(None, "shard", None),
        P(),
        P(),
        P(("grp", "shard"), None),
    )
    out_specs = (
        P(("grp", "shard"), None),
        P(("grp", "shard"), None),
        P(None, "shard", "grp", None),
    )
    return jax.shard_map(
        on_device, mesh=mesh, in_specs=in_specs, out_specs=out_specs, check_vma=False
    )
```

profile of v0, /device:TPU:0, one launch (start us, length us, event | category | flops | bytes accessed | tf_op | source)
XLA Modules:
  0.0 300.2 jit_solution(15566653151355944525)
XLA Ops:
  7.2 0.0 copy-start
  7.2 0.0 reduce-scatter.2.cloned.1.call-start
  7.2 0.7 compare_select_fusion.4
  8.0 0.1 copy.43
  8.1 0.1 reshape.222
  8.2 0.7 dynamic-slice_bitcast_fusion.2
  8.9 3.3 %gather_fusion.1 = s32[512]{0:T(512)S(1)} fusion(s32[32]{0:T(128)S(1)} %dynamic-slice_bitcast_fusion.2, s32[1024]{0:T(1024)S(1)} %pad_clamp_fusion.1), kind=kCustom, calls=%fused_computation.1 | custom fusion | bytes 6144 | tf_op jit(solution)/shard_map/gather | solution.py:82
  12.2 0.1 reshape.221
  12.4 0.1 copy.44
  12.5 14.5 %all_gather.6 = s32[1024,1,4]{0,2,1:T(4,128)S(1)} all-gather(s32[128,1,4]{0,2,1:T(4,128)S(1)} %fusion.15), channel_id=1, replica_groups=mesh['grp'=4,'shard'=8] {'shard'}, dimensions={0}, use_global_device_ids=true | all-gather | bytes 18432 | tf_op jit(solution)/shard_map/all_gather | solution.py:83
  26.9 0.3 broadcast_in_dim.110
  27.2 0.0 copy-start.8
  27.2 0.0 copy-start.3
  27.2 0.0 copy-start.7
  27.3 162.0 %while.30 = (s32[]{:T(128)}, f32[1024,1,128]{2,1,0:T(1,128)S(1)}, s32[1024,1,4]{0,2,1:T(4,128)S(1)}, s32[]{:T(128)}, f32[1,7872,128]{2,1,0:T(8,128)}, /*index=5*/s32[]{:T(128)}, s32[]{:T(128)}, s32[]{:T(128)}, s32[]{:T(128)}) while((s32[]{:T(128)}, f32[1024,1,128]{2,1,0:T(1,128)S(1)}, s32[1024,1,4]{0,2,1:T(4,128)S(1)}, s32[]{:T(128)}, ...), condition=%wide.region_2.3_spmd, body=%wide.region_0.2_spmd.sunk | while | flops 552966 | bytes 4325543 | solution.py:41
  27.3 0.1 copy.51
  27.5 0.2 reshape.281
  27.7 76.2 %gather_fusion = f32[2048,128]{1,0:T(8,128)S(1)} fusion(f32[1,7872,128]{2,1,0:T(8,128)} %get-tuple-element.379, s32[2048]{0:T(1024)S(1)} %reshape.281), kind=kCustom, calls=%fused_computation.clone.1 | custom fusion | bytes 2113536 | tf_op jit(solution)/shard_map/while/body/eval_jaxpr/gather | solution.py:35
  103.9 0.2 copy.52
  104.1 2.9 select_reduce_fusion.2
  107.0 0.3 add_dynamic-update-slice_fusion.2
  107.4 0.1 copy.51
  107.5 0.2 reshape.281
  107.7 78.1 %gather_fusion = f32[2048,128]{1,0:T(8,128)S(1)} fusion(f32[1,7872,128]{2,1,0:T(8,128)} %get-tuple-element.379, s32[2048]{0:T(1024)S(1)} %reshape.281), kind=kCustom, calls=%fused_computation.clone.1 | custom fusion | bytes 2113536 | tf_op jit(solution)/shard_map/while/body/eval_jaxpr/gather | solution.py:35
  185.8 0.2 copy.52
  186.0 2.9 select_reduce_fusion.2
  188.9 0.3 add_dynamic-update-slice_fusion.2
  189.2 0.8 copy-done.1
  190.0 0.0 reduce-scatter.2.cloned.1.call-update
  190.1 0.2 dynamic-slice_reduce_fusion
  190.3 0.1 add_remainder_fusion.1
  190.3 0.1 rem.69
  190.4 0.1 dynamic-slice_bitcast_fusion.1
  190.5 0.1 compare_select_fusion.3
  190.6 0.1 reshape.232
  190.7 28.3 %reduce-scatter.2.cloned.1.call-done = f32[128,1,128]{2,0,1:T(8,128)} async-done(((f32[1024,1,128]{2,0,1:T(8,128)}), f32[128,1,128]{2,0,1:T(8,128)}) %reduce-scatter.2.cloned.1.call-update) | async-done | bytes 65552 | tf_op jit(solution)/shard_map/reduce_scatter | solution.py:85
  219.0 0.9 fusion.11
  220.0 0.0 copy-start.4
  220.0 0.0 copy-start.5
  220.0 1.1 add_multiply_fusion
  221.1 0.5 convolution_bitcast_fusion
  221.7 0.1 convert_multiply_fusion
  221.8 14.9 %all-gather = f32[1024,128]{1,0:T(8,128)S(1)} all-gather(f32[128,128]{1,0:T(8,128)S(1)} %convert_multiply_fusion), channel_id=2, replica_groups=mesh['grp'=4,'shard'=8] {'shard'}, dimensions={0}, use_global_device_ids=true | all-gather | bytes 589824 | tf_op jit(solution)/shard_map/all_gather | solution.py:115
  236.7 2.1 broadcast_in_dim.113
  238.9 40.0 %while.31 = (s32[]{:T(128)}, f32[1,7872,128]{2,1,0:T(8,128)}, s32[1024,1,4]{0,2,1:T(4,128)S(1)}, s32[]{:T(128)}, f32[1024,1,128]{2,0,1:T(8,128)S(1)}, /*index=5*...) while((s32[]{:T(128)}, f32[1,7872,128]{2,1,0:T(8,128)}, ...), condition=%wide.region_7.8_spmd, body=%wide.region_5.7_spmd.sunk | while | flops 565254 | bytes 5099719 | solution.py:67
  238.9 0.1 fusion.33
  239.0 0.1 fusion.34
  239.1 0.1 copy.53
  239.2 0.2 reshape.284
  239.4 0.2 copy.54
  239.6 2.3 broadcast_select_fusion.5
  241.9 16.8 %scatter_fusion = f32[7872,128]{1,0:T(8,128)} fusion(f32[7872,128]{1,0:T(8,128)} %bitcast.73, s32[2048]{0:T(1024)S(1)} %reshape.284, f32[2048,128]{1,0:T(8,128)S(1)} %bitcast.77), kind=kCustom, calls=%fused_computation.3.clone.1 | custom fusion | flops 262144 | bytes 3153920 | tf_op jit(solution)/shard_map/while
  258.7 0.1 fusion.33
  258.8 0.1 fusion.34
  258.9 0.1 copy.53
  259.0 0.2 reshape.284
  259.3 0.2 copy.54
  259.5 2.3 broadcast_select_fusion.5
  261.8 17.2 %scatter_fusion = f32[7872,128]{1,0:T(8,128)} fusion(f32[7872,128]{1,0:T(8,128)} %bitcast.73, s32[2048]{0:T(1024)S(1)} %reshape.284, f32[2048,128]{1,0:T(8,128)S(1)} %bitcast.77), kind=kCustom, calls=%fused_computation.3.clone.1 | custom fusion | flops 262144 | bytes 3153920 | tf_op jit(solution)/shard_map/while
  278.9 3.5 %gather_fusion.2 = f32[256,128]{1,0:T(8,128)} fusion(f32[7872,128]{1,0:T(8,128)} %bitcast.75, s32[1024]{0:T(1024)S(1)} %pad_clamp_fusion), kind=kCustom, calls=%fused_computation.2 | custom fusion | bytes 263168 | tf_op jit(solution)/shard_map/gather | solution.py:126
  282.4 3.5 %all-to-all-start = ((f32[1,4,64,128]{3,2,0,1:T(8,128)}), f32[1,4,64,128]{3,2,0,1:T(8,128)S(1)}, u32[]{:S(2)}, u32[]{:S(2)}) async-start(f32[1,4,64,128]{3,2,0,1:T(8,128)} %bitcast.22), calls=%async_computation.1 | async-start | bytes 262144 | tf_op jit(solution)/shard_map/all_to_all | solution.py:127
  285.9 0.9 convolution_add_fusion.1
  286.8 4.2 %all-to-all-done = f32[1,4,64,128]{3,2,0,1:T(8,128)S(1)} async-done(((f32[1,4,64,128]{3,2,0,1:T(8,128)}), f32[1,4,64,128]{3,2,0,1:T(8,128)S(1)}, u32[]{:S(2)}, u32[]{:S(2)}) %all-to-all-start) | async-done | bytes 131104 | tf_op jit(solution)/shard_map/all_to_all | solution.py:127
  291.0 2.4 scatter_custom_fusion.1
  (34 shorter events, 0.3 us)
Async XLA Ops:
  7.2 212.8 %copy-start = (bf16[128,1024]{1,0:T(8,128)(2,1)S(1)}, bf16[128,1024]{1,0:T(8,128)(2,1)}, u32[]{:S(2)}) copy-start(bf16[128,1024]{1,0:T(8,128)(2,1)} %param.15) | copy-start | bytes 786436
  7.2 211.9 %reduce-scatter.2.cloned.1.call-start = ((), (), s32[]{:S(2)}) async-start(), calls=%async_computation.2 | async-start | bytes 589824 | tf_op jit(solution)/shard_map/reduce_scatter | solution.py:85
  8.9 3.5 %copy-start.6 = (s32[128,1,4]{0,2,1:T(4,128)S(1)}, s32[128,1,4]{0,2,1:T(4,128)}, u32[]{:S(2)}) copy-start(s32[128,1,4]{0,2,1:T(4,128)} %param.12) | copy-start | bytes 6148
  27.2 162.8 %copy-start.8 = (s32[4,32]{1,0:T(4,128)S(1)}, s32[4,32]{1,0:T(4,128)}, u32[]{:S(2)}) copy-start(s32[4,32]{1,0:T(4,128)} %param.13) | copy-start | bytes 1540
  27.2 191.8 %copy-start.3 = (bf16[128,128]{1,0:T(8,128)(2,1)S(1)}, bf16[128,128]{1,0:T(8,128)(2,1)}, u32[]{:S(2)}) copy-start(bf16[128,128]{1,0:T(8,128)(2,1)} %param.11) | copy-start | bytes 98308
  27.2 192.8 %copy-start.7 = (f32[1,1024]{1,0:T(1,128)S(1)}, f32[1,1024]{1,0:T(1,128)}, u32[]{:S(2)}) copy-start(f32[1,1024]{1,0:T(1,128)} %param.16) | copy-start | bytes 12292
  27.3 192.8 %copy-start.9 = (f32[128,1024]{1,0:T(8,128)S(1)}, f32[128,1024]{1,0:T(8,128)}, u32[]{:S(2)}) copy-start(f32[128,1024]{1,0:T(8,128)} %param.17) | copy-start | bytes 1572868
  189.2 0.8 copy-start.1
  220.0 18.8 %copy-start.4 = (s32[2]{0:T(128)S(1)}, s32[2]{0:T(128)}, u32[]{:S(2)}) copy-start(s32[2]{0:T(128)} %constant.362) | copy-start | bytes 28
  220.0 18.8 %copy-start.5 = (s32[2]{0:T(128)S(1)}, s32[2]{0:T(128)}, u32[]{:S(2)}) copy-start(s32[2]{0:T(128)} %constant.361) | copy-start | bytes 28
  238.9 47.1 %copy-start.2 = (f32[128,1,128]{2,0,1:T(8,128)S(1)}, f32[128,1,128]{2,0,1:T(8,128)}, u32[]{:S(2)}) copy-start(f32[128,1,128]{2,0,1:T(8,128)} %reduce-scatter.2.cloned.1.call-done) | copy-start | bytes 196612
  282.4 8.6 %all-to-all-start = ((f32[1,4,64,128]{3,2,0,1:T(8,128)}), f32[1,4,64,128]{3,2,0,1:T(8,128)S(1)}, u32[]{:S(2)}, u32[]{:S(2)}) async-start(f32[1,4,64,128]{3,2,0,1:T(8,128)} %bitcast.22), calls=%async_computation.1 | async-start | bytes 262144 | tf_op jit(solution)/shard_map/all_to_all | solution.py:127
Sparse Core Ops, SparseCore 0:
  190.2 28.8 reduce-scatter.1
where the time goes:
time: 302 us; the launch traced here: 300 us
  local copies, waits for them, and re-layouts  168 us (56%)
  other arithmetic  49.8 us (16%)
  waiting for transfers between devices  32.5 us (11%)
  blocking collectives  29.4 us (10%)
  between operations  14.2 us (5%)
  starting transfers between devices  3.58 us (1%)
    gather x2, local copies, waits for them, and re-layouts, pool_step(): fetched = tables[table_ids, jnp.clip(local, 0, span_rows - 1)]  154 us
    while x8, other arithmetic  34.3 us
    reduce_scatter x1, waiting for transfers between devices, on_device(): lax.psum_scatter(pool_lookups(tables, picked, offset), 'shard', scatter_d...  28.3 us
    all_gather x1, blocking collectives, on_device(): lax.all_gather(pooled_grad, 'shard', axis=0, tiled=True)  14.9 us
    all_gather x1, blocking collectives, on_device(): group_idx = lax.all_gather(own_rows, 'shard', axis=0, tiled=True)  14.5 us
  transfers between devices with their start and end apart: 2, of which 2 were waited for; matrix products, arithmetic and copies ran while one was open for 0% of the time, Pallas kernels for 0%

commit v1 on v0

v1 whole, which is shorter than its diff:
```python
import functools

import jax
import jax.numpy as jnp
from jax import lax
from jax.experimental import pallas as pl
from jax.experimental.pallas import tpu as pltpu
from jax.sharding import PartitionSpec as P

HOT = 64
MESH = pl.DeviceIdType.MESH
VMEM = pltpu.VMEM
DMA = pltpu.SemaphoreType.DMA


def split_two(value):
    high = value.astype(jnp.bfloat16)
    low = (value - high.astype(jnp.float32)).astype(jnp.bfloat16)
    return high, low


def exchange_kernel(
    groups, shards, window,
    starts_ref, lookups_ref, bottom_ref, tables_ref, dense_ref, pairs_ref, cot_ref,
    act_ref, bottom_grad_ref, hot_out_ref,
    tab, looks, bottoms, counts, part_far, part_own, from_sib, arrived, pair_all,
    weighted, preact_ref, half_ref, grad_send, grad_recv,
    tab_sem, look_send, look_recv, bot_send, bot_recv, sib_send, sib_recv,
    sum_send, sum_recv, pair_send, pair_recv, grp_send, grp_recv,
):
    bag, batch = lookups_ref.shape
    width = bottom_ref.shape[1]
    hidden = cot_ref.shape[1]
    chips = shards // 2
    hot_rows = groups * HOT
    me = lax.axis_index("shard")
    grp = lax.axis_index("grp")
    core = lax.rem(me, 2)
    chip = lax.div(me, 2)
    sib = chip * 2 + 1 - core

    def remote(src, dst, send, recv, **where):
        return pltpu.make_async_remote_copy(
            src_ref=src, dst_ref=dst, send_sem=send, recv_sem=recv,
            device_id=where, device_id_type=MESH,
        )

    tab_copies = []
    for win in range(groups):
        first = win * window
        tab_copies.append(pltpu.make_async_copy(
            tables_ref.at[0, pl.ds(first, window)], tab.at[win, pl.ds(0, window)], tab_sem.at[2 * win]))
        tab_copies.append(pltpu.make_async_copy(
            tables_ref.at[0, pl.ds(first, HOT)], tab.at[win, pl.ds(window, HOT)], tab_sem.at[2 * win + 1]))
    for copy in tab_copies:
        copy.start()

    barrier = pltpu.get_barrier_semaphore()
    peers = [lax.rem(me + step, shards) for step in range(1, shards)]
    grp_peers = [lax.rem(grp + step, groups) for step in range(1, groups)]
    for peer in peers:
        pl.semaphore_signal(barrier, inc=1, device_id={"shard": peer}, device_id_type=MESH)
    for peer in grp_peers:
        pl.semaphore_signal(barrier, inc=1, device_id={"grp": peer}, device_id_type=MESH)
    looks[me] = lookups_ref[...]
    bottom_wide = bottom_ref[...].astype(jnp.float32)
    bottoms[me] = bottom_wide
    pl.semaphore_wait(barrier, len(peers) + len(grp_peers))

    sends = []
    for peer in peers:
        copy = remote(looks.at[me], looks.at[me], look_send.at[peer], look_recv.at[me], shard=peer)
        copy.start()
        sends.append(copy)
    far_chips = [lax.rem(chip + step, chips) for step in range(1, chips)]
    for peer in [other * 2 + core for other in far_chips] + [sib]:
        copy = remote(bottoms.at[me], bottoms.at[me], bot_send.at[peer], bot_recv.at[me], shard=peer)
        copy.start()
        sends.append(copy)

    preact_ref[...] = jnp.dot(bottom_ref[...], dense_ref[...], preferred_element_type=jnp.float32)

    for copy in tab_copies:
        copy.wait()
    flipped = []
    for win in range(groups):
        start = starts_ref[grp, me * groups + win]
        flipped.append(tab[win, pl.ds(start, HOT), :].T)
    hot_high, hot_low = split_two(jnp.concatenate(flipped, axis=1))
    hot_both = jnp.concatenate([hot_high, hot_low], axis=0)

    slot = lax.broadcasted_iota(jnp.int32, (hot_rows, batch), 0)
    wanted = slot + lax.div(slot, HOT) * (window - HOT) + me * (groups * window)

    def partial_sum(source):
        rows = looks[source]
        hits = jnp.zeros((hot_rows, batch), jnp.float32)
        for place in range(bag):
            hits = hits + jnp.where(rows[place:place + 1, :] == wanted, 1.0, 0.0)
        hits = hits.astype(jnp.bfloat16)
        counts[:, pl.ds(pl.multiple_of(source * batch, batch), batch)] = hits
        both = jnp.dot(hot_both, hits, preferred_element_type=jnp.float32)
        return both[:width] + both[width:]

    def look_wait(source):
        remote(looks.at[source], looks.at[source], look_send.at[source], look_recv.at[source],
               shard=source).wait_recv()

    for other in far_chips + [chip]:
        source = other * 2 + 1 - core
        look_wait(source)
        part_far[other] = partial_sum(source)
        copy = remote(part_far.at[other], from_sib.at[other], sib_send.at[other], sib_recv.at[other], shard=sib)
        copy.start()
        sends.append(copy)
    for other in far_chips:
        look_wait(other * 2 + core)
        part_own[other] = partial_sum(other * 2 + core)
    part_own[chip] = partial_sum(me)

    def sib_wait(other):
        remote(part_far.at[other], from_sib.at[other], sib_send.at[other], sib_recv.at[other],
               shard=sib).wait_recv()

    for other in far_chips:
        sib_wait(other)
        part_own[other] = part_own[other] + from_sib[other]
        copy = remote(part_own.at[other], arrived.at[chip], sum_send.at[other], sum_recv.at[chip],
                      shard=other * 2 + core)
        copy.start()
        sends.append(copy)

    def bottom_wait(source):
        remote(bottoms.at[source], bottoms.at[source], bot_send.at[source], bot_recv.at[source],
               shard=sib).wait_recv()

    for other in far_chips:
        source = other * 2 + core
        bottom_wait(source)
        copy = remote(bottoms.at[source], bottoms.at[source], bot_send.at[other * 2 + 1 - core],
                      bot_recv.at[source], shard=sib)
        copy.start()
        sends.append(copy)

    sib_wait(chip)
    pooled_flip = part_own[chip] + from_sib[chip]
    for other in far_chips:
        remote(part_own.at[other], arrived.at[other], sum_send.at[other], sum_recv.at[other],
               shard=other * 2 + core).wait_recv()
        pooled_flip = pooled_flip + arrived[other]
    pooled = pooled_flip.T
    dots = jnp.sum(bottom_wide * pooled, axis=1, keepdims=True)

    chunk = 256 if hidden % 256 == 0 else hidden
    lanes = 128 if chunk % 128 == 0 else chunk
    running = jnp.zeros((batch, lanes), jnp.float32)
    for first in range(0, hidden, chunk):
        cut = slice(first, first + chunk)
        weights = pairs_ref[0:1, cut]
        preact = preact_ref[:, cut] + dots * weights
        sig = jax.nn.sigmoid(preact)
        preact_ref[:, cut] = preact * sig
        pre_grad = cot_ref[:, cut] * sig * (1.0 + preact * (1.0 - sig))
        half_ref[:, cut] = pre_grad.astype(jnp.bfloat16)
        product = pre_grad * weights
        for lane in range(0, chunk, lanes):
            running = running + product[:, lane:lane + lanes]
    pair_col = jnp.sum(running, axis=1, keepdims=True)
    pair_row = jnp.broadcast_to(pair_col, (batch, 128)).T[0:8]
    pair_all[me] = pair_row
    for peer in peers:
        copy = remote(pair_all.at[me], pair_all.at[me], pair_send.at[peer], pair_recv.at[me], shard=peer)
        copy.start()
        sends.append(copy)

    act_ref[...] = preact_ref[...].astype(jnp.bfloat16)
    bottom_grad_ref[...] = lax.dot_general(
        half_ref[...], dense_ref[...], (((1,), (1,)), ((), ())), preferred_element_type=jnp.float32
    ) + pair_col * pooled

    for other in far_chips:
        bottom_wait(other * 2 + 1 - core)
    bottom_wait(sib)
    for peer in peers:
        remote(pair_all.at[peer], pair_all.at[peer], pair_send.at[peer], pair_recv.at[peer],
               shard=peer).wait_recv()
    for source in range(shards):
        column = jnp.broadcast_to(pair_all[source][0:1, :], (width, batch)).T
        high, low = split_two(bottoms[source] * column)
        weighted[source * batch:(source + 1) * batch, 0:width] = high
        weighted[source * batch:(source + 1) * batch, width:2 * width] = low
    per_dot = 4 if groups % 4 == 0 else 1
    for win in range(0, groups, per_dot):
        both = jnp.dot(counts[win * HOT:(win + per_dot) * HOT, :], weighted[...],
                       preferred_element_type=jnp.float32)
        summed = both[:, :width] + both[:, width:]
        for step in range(per_dot):
            grad_send[win + step] = summed[step * HOT:(step + 1) * HOT]
    for peer in grp_peers:
        copy = remote(grad_send.at[peer], grad_recv.at[grp], grp_send.at[peer], grp_recv.at[grp], grp=peer)
        copy.start()
        sends.append(copy)
    hot_out_ref[grp] = grad_send[grp]
    for peer in grp_peers:
        remote(grad_send.at[peer], grad_recv.at[peer], grp_send.at[peer], grp_recv.at[peer],
               grp=peer).wait_recv()
        hot_out_ref[peer] = grad_recv[peer]
    for copy in sends:
        copy.wait_send()


def place_kernel(groups, window, starts_ref, hot_ref, act_in, bottom_in, act_out, bottom_out, table_out,
                 spread, sem):
    me = lax.axis_index("shard")
    grp = lax.axis_index("grp")
    act_copy = pltpu.make_async_copy(act_in, act_out, sem.at[0])
    bottom_copy = pltpu.make_async_copy(bottom_in, bottom_out, sem.at[1])
    act_copy.start()
    bottom_copy.start()
    spread[...] = jnp.zeros_like(spread)
    for source in range(groups):
        start = starts_ref[source, me * groups + grp]
        spread[pl.ds(start, HOT), :] += hot_ref[source]
    spread[0:HOT, :] += spread[window:window + HOT, :]
    table_copy = pltpu.make_async_copy(spread.at[pl.ds(0, window)], table_out.at[0, 0], sem.at[2])
    table_copy.start()
    act_copy.wait()
    bottom_copy.wait()
    table_copy.wait()


def on_device(groups, shards, bottom_out, lookups, starts, tables, top_dense, top_pairs, cotangent):
    batch, width = bottom_out.shape
    hidden = cotangent.shape[1]
    bag = lookups.shape[2]
    window = tables.shape[1] // groups
    hot_rows = groups * HOT
    chips = shards // 2
    flipped = lookups[:, 0, :].T
    in_vmem = pl.BlockSpec(memory_space=VMEM)
    in_smem = pl.BlockSpec(memory_space=pltpu.SMEM)
    anywhere = pl.BlockSpec(memory_space=pl.ANY)
    f32, bf16 = jnp.float32, jnp.bfloat16
    blocks = VMEM((chips, width, batch), f32)
    act, bottom_grad, hot_grad = pl.pallas_call(
        functools.partial(exchange_kernel, groups, shards, window),
        out_shape=(
            jax.ShapeDtypeStruct((batch, hidden), bf16),
            jax.ShapeDtypeStruct((batch, width), f32),
            jax.ShapeDtypeStruct((groups, HOT, width), f32),
        ),
        in_specs=[in_smem, in_vmem, in_vmem, anywhere, in_vmem, in_vmem, in_vmem],
        out_specs=(in_vmem, in_vmem, in_vmem),
        scratch_shapes=[
            VMEM((groups, window + HOT, width), f32),
            VMEM((shards, bag, batch), jnp.int32),
            VMEM((shards, batch, width), f32),
            VMEM((hot_rows, shards * batch), bf16),
            blocks, blocks, blocks, blocks,
            VMEM((shards, 8, 128), f32),
            VMEM((shards * batch, 2 * width), bf16),
            VMEM((batch, hidden), f32),
            VMEM((batch, hidden), bf16),
            VMEM((groups, HOT, width), f32),
            VMEM((groups, HOT, width), f32),
            DMA((2 * groups,)),
            DMA((shards,)), DMA((shards,)), DMA((shards,)), DMA((shards,)),
            DMA((chips,)), DMA((chips,)), DMA((chips,)), DMA((chips,)),
            DMA((shards,)), DMA((shards,)), DMA((groups,)), DMA((groups,)),
        ],
        compiler_params=pltpu.CompilerParams(
            collective_id=0, has_side_effects=True, vmem_limit_bytes=48 * 1024 * 1024
        ),
    )(starts, flipped, bottom_out, tables, top_dense, top_pairs, cotangent)
    return pl.pallas_call(
        functools.partial(place_kernel, groups, window),
        out_shape=(
            jax.ShapeDtypeStruct((batch, hidden), bf16),
            jax.ShapeDtypeStruct((batch, width), f32),
            jax.ShapeDtypeStruct((1, 1, window, width), f32),
        ),
        in_specs=[in_smem, in_vmem, in_vmem, in_vmem],
        out_specs=(anywhere, anywhere, anywhere),
        scratch_shapes=[VMEM((window + HOT, width), f32), DMA((3,))],
        compiler_params=pltpu.CompilerParams(vmem_limit_bytes=16 * 1024 * 1024),
    )(starts, hot_grad, act, bottom_grad)


def solution(mesh):
    groups, shards = mesh.shape["grp"], mesh.shape["shard"]
    in_specs = (
        P(("grp", "shard"), None),
        P(("grp", "shard"), None, None),
        P(),
        P(None, "shard", None),
        P(),
        P(),
        P(("grp", "shard"), None),
    )
    out_specs = (
        P(("grp", "shard"), None),
        P(("grp", "shard"), None),
        P(None, "shard", "grp", None),
    )
    return jax.shard_map(
        functools.partial(on_device, groups, shards),
        mesh=mesh, in_specs=in_specs, out_specs=out_specs, check_vma=False,
    )
```

time: 302 us -> 40.1 us (0.13)
  local copies, waits for them, and re-layouts: 168 us -> 6.93 us
  other arithmetic: 49.8 us -> 0 us
  waiting for transfers between devices: 32.5 us -> 0 us
  Pallas kernels: 0 us -> 32.2 us
  blocking collectives: 29.4 us -> 0 us
  between operations: 14.2 us -> 0.66 us
  starting transfers between devices: 3.58 us -> 0 us
    gather x6 -> x0, local copies, waits for them, and re-layouts: 161 us -> none  [the longest x2 154 us: pool_step(): fetched = tables[table_ids, jnp.clip(local, 0, span_rows - 1)]]
    while x8 -> x0, other arithmetic: 34.3 us -> none
    pallas_call x0 -> x2, Pallas kernels: none -> 32.2 us  [the longest x1 30.5 us: on_device(): pl.pallas_call(functools.partial(exchange_kernel, groups, shards, window)...]
    all_gather x2 -> x0, blocking collectives: 29.4 us -> none  [the longest x1 14.9 us: on_device(): lax.all_gather(pooled_grad, 'shard', axis=0, tiled=True)]
    reduce_scatter x1 -> x0, waiting for transfers between devices: 28.3 us -> none  [on_device(): lax.psum_scatter(pool_lookups(tables, picked, offset), 'shard', scatter_d...]
    reduce_sum x3 -> x0, other arithmetic: 6.79 us -> none  [the longest x2 5.84 us: pool_step(): summed = jnp.sum(jnp.where(inside[..., None], fetched, 0.0), axis=2)]
    unnamed x20 -> x14, local copies, waits for them, and re-layouts: 0.84 us -> 6.93 us
    select_n x5 -> x0, other arithmetic: 5.41 us -> none  [the longest x2 4.59 us: add_step(): updates = jnp.where(inside[..., None], grads_block[:, :, None, :], 0.0)]
  transfers between devices with their start and end apart: 2 -> 0, of which waited for: 2 -> 0; matrix products, arithmetic and copies ran while one was open for 0% -> 0% of each run, Pallas kernels for 0% -> 0%
where the time goes in v1:
time: 40.1 us; the launch traced here: 39.8 us
  Pallas kernels  32.2 us (80%)
  local copies, waits for them, and re-layouts  6.93 us (17%)
  between operations  0.66 us (2%)
    pallas_call x1, Pallas kernels, on_device(): pl.pallas_call(functools.partial(exchange_kernel, groups, shards, window)...  30.5 us
    unnamed x14, local copies, waits for them, and re-layouts  6.93 us
    pallas_call x1, Pallas kernels, on_device(): pl.pallas_call(functools.partial(place_kernel, groups, window), out_shape...  1.65 us

profile of v1, /device:TPU:0, one launch (start us, length us, event | category | flops | bytes accessed | tf_op | source)
XLA Modules:
  0.0 39.8 jit_solution(4075898024774441419)
XLA Ops:
  0.6 0.0 copy-start
  0.6 2.1 %copy-done = f32[1,7872,128]{2,1,0:T(8,128)S(1)} copy-done((f32[1,7872,128]{2,1,0:T(8,128)S(1)}, f32[1,7872,128]{2,1,0:T(8,128)}, u32[]{:S(2)}) %copy-start) | copy-done | bytes 4030488
  2.8 0.0 copy-start.1
  2.8 1.0 %copy-done.1 = f32[128,1024]{1,0:T(8,128)S(1)} copy-done((f32[128,1024]{1,0:T(8,128)S(1)}, f32[128,1024]{1,0:T(8,128)}, u32[]{:S(2)}) %copy-start.1) | copy-done | bytes 524312
  3.8 0.0 copy-start.2
  3.8 0.9 %copy-done.2 = bf16[128,1024]{1,0:T(8,128)(2,1)S(1)} copy-done((bf16[128,1024]{1,0:T(8,128)(2,1)S(1)}, bf16[128,1024]{1,0:T(8,128)(2,1)}, u32[]{:S(2)}) %copy-start.2) | copy-done | bytes 262168
  4.8 0.0 copy-start.3
  4.8 0.8 %copy-done.3 = bf16[128,128]{1,0:T(8,128)(2,1)S(1)} copy-done((bf16[128,128]{1,0:T(8,128)(2,1)S(1)}, bf16[128,128]{1,0:T(8,128)(2,1)}, u32[]{:S(2)}) %copy-start.3) | copy-done | bytes 32792
  5.5 0.0 copy-start.4
  5.5 0.7 %copy-done.4 = s32[4,32]{1,0:T(4,128)S(1)} copy-done((s32[4,32]{1,0:T(4,128)S(1)}, s32[4,32]{1,0:T(4,128)}, u32[]{:S(2)}) %copy-start.4) | copy-done | bytes 536
  6.2 0.0 copy-start.5
  6.2 0.7 %copy-done.5 = f32[1,1024]{1,0:T(1,128)S(1)} copy-done((f32[1,1024]{1,0:T(1,128)S(1)}, f32[1,1024]{1,0:T(1,128)}, u32[]{:S(2)}) %copy-start.5) | copy-done | bytes 4120
  6.9 0.0 copy-start.6
  6.9 0.7 %copy-done.6 = s32[128,1,4]{0,2,1:T(4,128)S(1)} copy-done((s32[128,1,4]{0,2,1:T(4,128)S(1)}, s32[128,1,4]{0,2,1:T(4,128)}, u32[]{:S(2)}) %copy-start.6) | copy-done | bytes 2072
  7.6 30.5 %shard_map.94 = (bf16[128,1024]{1,0:T(8,128)(2,1)S(1)}, f32[128,128]{1,0:T(8,128)S(1)}, f32[4,64,128]{2,1,0:T(8,128)S(1)}) custom-call(s32[4,32]{1,0:T(4,128)S(1)} %copy-done.4, s32[4,128]{1,0:T(4,128)S(1)} %bitcast.3, bf16[128,128]{1,0:T(8,128)(2,1)S(1)} %copy-done.3, f32[1,7872,128]{2,1,0:T(8,128)S(1)} %copy-done, bf16[128,1024]{1,0:T(8,128)(2,1)S(1)} %copy-done.2, ...), custom_call_target="tpu_custom_call" | custom-call | tf_op jit(solution)/shard_map/pallas_call | solution.py:245
  38.1 1.7 %shard_map.95 = (bf16[128,1024]{1,0:T(8,128)(2,1)}, f32[128,128]{1,0:T(8,128)}, f32[1,1,1968,128]{3,2,1,0:T(8,128)}) custom-call(s32[4,32]{1,0:T(4,128)S(1)} %copy-done.4, f32[4,64,128]{2,1,0:T(8,128)S(1)} %get-tuple-element.6.hot_ref, bf16[128,1024]{1,0:T(8,128)(2,1)S(1)} %get-tuple-element.7.act_in, f32[128,128]{1,0:T(8,128)S(1)} %get-tuple-element.8.bottom_in), custom_call_target="tpu_custom_call" | custom-call | tf_op jit(solution)/shard_map/pallas_call | solution.py:275
Async XLA Ops:
  0.6 2.1 %copy-start = (f32[1,7872,128]{2,1,0:T(8,128)S(1)}, f32[1,7872,128]{2,1,0:T(8,128)}, u32[]{:S(2)}) copy-start(f32[1,7872,128]{2,1,0:T(8,128)} %tables_ref.1) | copy-start | bytes 12091396
  2.8 1.0 %copy-start.1 = (f32[128,1024]{1,0:T(8,128)S(1)}, f32[128,1024]{1,0:T(8,128)}, u32[]{:S(2)}) copy-start(f32[128,1024]{1,0:T(8,128)} %cot_ref.1) | copy-start | bytes 1572868
  3.8 0.9 %copy-start.2 = (bf16[128,1024]{1,0:T(8,128)(2,1)S(1)}, bf16[128,1024]{1,0:T(8,128)(2,1)}, u32[]{:S(2)}) copy-start(bf16[128,1024]{1,0:T(8,128)(2,1)} %dense_ref.1) | copy-start | bytes 786436
  4.8 0.8 %copy-start.3 = (bf16[128,128]{1,0:T(8,128)(2,1)S(1)}, bf16[128,128]{1,0:T(8,128)(2,1)}, u32[]{:S(2)}) copy-start(bf16[128,128]{1,0:T(8,128)(2,1)} %bottom_ref.1) | copy-start | bytes 98308
  5.5 0.7 %copy-start.4 = (s32[4,32]{1,0:T(4,128)S(1)}, s32[4,32]{1,0:T(4,128)}, u32[]{:S(2)}) copy-start(s32[4,32]{1,0:T(4,128)} %starts_ref.3) | copy-start | bytes 1540
  6.2 0.7 %copy-start.5 = (f32[1,1024]{1,0:T(1,128)S(1)}, f32[1,1024]{1,0:T(1,128)}, u32[]{:S(2)}) copy-start(f32[1,1024]{1,0:T(1,128)} %pairs_ref.1) | copy-start | bytes 12292
  6.9 0.7 %copy-start.6 = (s32[128,1,4]{0,2,1:T(4,128)S(1)}, s32[128,1,4]{0,2,1:T(4,128)}, u32[]{:S(2)}) copy-start(s32[128,1,4]{0,2,1:T(4,128)} %param.8) | copy-start | bytes 6148

commit v2 on v1

v2 whole, which is shorter than its diff:
```python
import functools

import jax
import jax.numpy as jnp
from jax import lax
from jax.experimental import pallas as pl
from jax.experimental.pallas import tpu as pltpu
from jax.sharding import PartitionSpec as P

HOT = 64
VMEM_ALL = 67043328
MESH = pl.DeviceIdType.MESH
VMEM = pltpu.VMEM
DMA = pltpu.SemaphoreType.DMA


def split_two(value):
    high = value.astype(jnp.bfloat16)
    low = (value - high.astype(jnp.float32)).astype(jnp.bfloat16)
    return high, low


def exchange_kernel(
    groups, shards, window,
    starts_ref, lookups_ref, bottom_ref, tables_ref, dense_ref, pairs_ref, cot_ref,
    act_ref, bottom_grad_ref, hot_out_ref,
    starts, bottom, dense, pairs, cot,
    tab, looks, bottoms, counts, partial, from_sib, arrived, dots_all, pair_all,
    weighted, preact_ref, half_ref, act, bottom_grad, grad_send,
    load_sem, tab_sem, look_send, look_recv, bot_send, bot_recv, sib_send, sib_recv,
    sum_send, sum_recv, dots_send, dots_recv, pair_send, pair_recv, grp_send, grp_recv,
):
    bag, batch = lookups_ref.shape
    width = bottom_ref.shape[1]
    hidden = cot_ref.shape[1]
    chips = shards // 2
    hot_rows = groups * HOT
    me = lax.axis_index("shard")
    grp = lax.axis_index("grp")
    core = lax.rem(me, 2)
    chip = lax.div(me, 2)
    sib = chip * 2 + 1 - core

    def remote(src, dst, send, recv, **where):
        return pltpu.make_async_remote_copy(
            src_ref=src, dst_ref=dst, send_sem=send, recv_sem=recv,
            device_id=where, device_id_type=MESH,
        )

    barrier = pltpu.get_barrier_semaphore()
    peers = [lax.rem(me + step, shards) for step in range(1, shards)]
    grp_peers = [lax.rem(grp + step, groups) for step in range(1, groups)]
    for peer in peers:
        pl.semaphore_signal(barrier, inc=1, device_id={"shard": peer}, device_id_type=MESH)
    for peer in grp_peers:
        pl.semaphore_signal(barrier, inc=1, device_id={"grp": peer}, device_id_type=MESH)

    def load(src, dst, place):
        copy = pltpu.make_async_copy(src, dst, load_sem.at[place])
        copy.start()
        return copy

    bottom_load = load(bottom_ref, bottom, 0)
    look_load = load(lookups_ref, looks.at[me], 1)
    starts_load = load(starts_ref, starts, 2)
    dense_load = load(dense_ref, dense, 3)
    tab_copies = []
    for win in range(groups):
        first = win * window
        tab_copies.append(pltpu.make_async_copy(
            tables_ref.at[0, pl.ds(first, window)], tab.at[win, pl.ds(0, window)], tab_sem.at[2 * win]))
        tab_copies.append(pltpu.make_async_copy(
            tables_ref.at[0, pl.ds(first, HOT)], tab.at[win, pl.ds(window, HOT)], tab_sem.at[2 * win + 1]))
    for copy in tab_copies:
        copy.start()
    pairs_load = load(pairs_ref, pairs, 4)
    cot_load = load(cot_ref, cot, 5)

    bottom_load.wait()
    bottoms[me] = bottom[...].astype(jnp.float32).T
    look_load.wait()
    pl.semaphore_wait(barrier, len(peers) + len(grp_peers))

    sends = []

    def send(src, dst, send_sem, recv_sem, **where):
        copy = remote(src, dst, send_sem, recv_sem, **where)
        copy.start()
        sends.append(copy)

    far_chips = [lax.rem(chip + step, chips) for step in range(1, chips)]
    for peer in peers:
        send(looks.at[me], looks.at[me], look_send.at[peer], look_recv.at[me], shard=peer)
    for peer in [other * 2 + core for other in far_chips] + [sib]:
        send(bottoms.at[me], bottoms.at[me], bot_send.at[peer], bot_recv.at[me], shard=peer)

    dense_load.wait()
    preact_ref[...] = jnp.dot(bottom[...], dense[...], preferred_element_type=jnp.float32)

    starts_load.wait()
    for copy in tab_copies:
        copy.wait()
    flipped = []
    for win in range(groups):
        start = starts[grp, me * groups + win]
        flipped.append(tab[win, pl.ds(start, HOT), :].T)
    hot_high, hot_low = split_two(jnp.concatenate(flipped, axis=1))
    hot_both = jnp.concatenate([hot_high, hot_low], axis=0)

    slot = lax.broadcasted_iota(jnp.int32, (hot_rows, batch), 0)
    wanted = slot + lax.div(slot, HOT) * (window - HOT) + me * (groups * window)

    def pool(source):
        rows = looks[source]
        hits = jnp.zeros((hot_rows, batch), jnp.float32)
        for place in range(bag):
            hits = hits + jnp.where(rows[place:place + 1, :] == wanted, 1.0, 0.0)
        hits = hits.astype(jnp.bfloat16)
        counts[:, pl.ds(pl.multiple_of(source * batch, batch), batch)] = hits
        both = jnp.dot(hot_both, hits, preferred_element_type=jnp.float32)
        partial[source] = both[:width] + both[width:]

    def look_wait(source):
        remote(looks.at[source], looks.at[source], look_send.at[source], look_recv.at[source],
               shard=source).wait_recv()

    pool(me)
    for source in [sib] + [other * 2 + 1 - core for other in far_chips]:
        look_wait(source)
        pool(source)
        other = lax.div(source, 2)
        send(partial.at[source], from_sib.at[other], sib_send.at[other], sib_recv.at[other], shard=sib)
    for other in far_chips:
        look_wait(other * 2 + core)
        pool(other * 2 + core)

    def dot_row(source):
        return jnp.sum(partial[source] * bottoms[source], axis=0, keepdims=True)

    def bottom_wait(source):
        remote(bottoms.at[source], bottoms.at[source], bot_send.at[source], bot_recv.at[source],
               shard=sib).wait_recv()

    def dot_send(source):
        dots_all[source] = dot_row(source)
        send(dots_all.at[source], pair_all.at[0, me], dots_send.at[source], dots_recv.at[me], shard=source)

    bottom_wait(sib)
    dot_send(sib)
    near_first = []
    for step in range(1, chips // 2 + 1):
        near_first.append(lax.rem(chip + step, chips))
        if step != chips - step:
            near_first.append(lax.rem(chip + chips - step, chips))
    for other in near_first:
        source = other * 2 + core
        bottom_wait(source)
        send(bottoms.at[source], bottoms.at[source], bot_send.at[other * 2 + 1 - core],
             bot_recv.at[source], shard=sib)
        dot_send(source)
    for other in near_first:
        source = other * 2 + 1 - core
        bottom_wait(source)
        dot_send(source)
    dots = dot_row(me)

    def sib_wait(other):
        remote(from_sib.at[other], from_sib.at[other], sib_send.at[other], sib_recv.at[other],
               shard=sib).wait_recv()

    for other in far_chips:
        sib_wait(other)
        from_sib[other] = from_sib[other] + partial[other * 2 + core]
        send(from_sib.at[other], arrived.at[chip], sum_send.at[other], sum_recv.at[chip],
             shard=other * 2 + core)

    for peer in peers:
        remote(dots_all.at[peer], pair_all.at[0, peer], dots_send.at[peer], dots_recv.at[peer],
               shard=peer).wait_recv()
        dots = dots + pair_all[0, peer]
    dots_col = jnp.broadcast_to(dots, (batch, batch)).T[:, 0:1]

    pairs_load.wait()
    cot_load.wait()
    chunk = 256 if hidden % 256 == 0 else hidden
    lanes = 128 if chunk % 128 == 0 else chunk
    running = jnp.zeros((batch, lanes), jnp.float32)
    for first in range(0, hidden, chunk):
        cut = slice(first, first + chunk)
        weights = pairs[0:1, cut]
        preact = preact_ref[:, cut] + dots_col * weights
        sig = jax.nn.sigmoid(preact)
        preact_ref[:, cut] = preact * sig
        pre_grad = cot[:, cut] * sig * (1.0 + preact * (1.0 - sig))
        half_ref[:, cut] = pre_grad.astype(jnp.bfloat16)
        product = pre_grad * weights
        for lane in range(0, chunk, lanes):
            running = running + product[:, lane:lane + lanes]
    pair_col = jnp.sum(running, axis=1, keepdims=True)
    pair_all[1, me] = jnp.broadcast_to(pair_col, (batch, batch)).T[0:1]
    for peer in peers:
        send(pair_all.at[1, me], pair_all.at[1, me], pair_send.at[peer], pair_recv.at[me], shard=peer)

    act[...] = preact_ref[...].astype(jnp.bfloat16)
    act_store = load(act, act_ref, 6)
    bottom_dense = lax.dot_general(
        half_ref[...], dense[...], (((1,), (1,)), ((), ())), preferred_element_type=jnp.float32
    )

    def weigh(source):
        high, low = split_two(bottoms[source] * pair_all[1, source])
        where = pl.ds(pl.multiple_of(source * batch, batch), batch)
        weighted[0:width, where] = high
        weighted[width:2 * width, where] = low

    weigh(me)
    for peer in peers:
        remote(pair_all.at[1, peer], pair_all.at[1, peer], pair_send.at[peer], pair_recv.at[peer],
               shard=peer).wait_recv()
        weigh(peer)
    per_dot = 4 if groups % 4 == 0 else 1
    for win in range(0, groups, per_dot):
        both = lax.dot_general(
            counts[win * HOT:(win + per_dot) * HOT, :], weighted[...],
            (((1,), (1,)), ((), ())), preferred_element_type=jnp.float32)
        summed = both[:, :width] + both[:, width:]
        for step in range(per_dot):
            grad_send[win + step] = summed[step * HOT:(step + 1) * HOT]
    for peer in grp_peers:
        send(grad_send.at[peer], hot_out_ref.at[grp], grp_send.at[peer], grp_recv.at[grp], grp=peer)
    own_store = load(grad_send.at[grp], hot_out_ref.at[grp], 7)

    sib_wait(chip)
    pooled = partial[me] + from_sib[chip]
    for other in far_chips:
        remote(from_sib.at[other], arrived.at[other], sum_send.at[other], sum_recv.at[other],
               shard=other * 2 + core).wait_recv()
        pooled = pooled + arrived[other]
    bottom_grad[...] = bottom_dense + (pooled * pair_all[1, me]).T
    bottom_store = load(bottom_grad, bottom_grad_ref, 8)
    for peer in grp_peers:
        remote(grad_send.at[peer], hot_out_ref.at[peer], grp_send.at[peer], grp_recv.at[peer],
               grp=peer).wait_recv()
    act_store.wait()
    own_store.wait()
    bottom_store.wait()
    for copy in sends:
        copy.wait_send()


def place_kernel(groups, window, starts_ref, hot_ref, act_in, bottom_in, act_out, bottom_out, table_out,
                 spread, starts, hot, act, bottom, sem):
    me = lax.axis_index("shard")
    grp = lax.axis_index("grp")

    def copy(src, dst, place):
        started = pltpu.make_async_copy(src, dst, sem.at[place])
        started.start()
        return started

    hot_load = copy(hot_ref, hot, 0)
    starts_load = copy(starts_ref, starts, 1)
    act_load = copy(act_in, act, 2)
    bottom_load = copy(bottom_in, bottom, 3)
    spread[...] = jnp.zeros_like(spread)
    starts_load.wait()
    hot_load.wait()
    for source in range(groups):
        start = starts[source, me * groups + grp]
        spread[pl.ds(start, HOT), :] += hot[source]
    spread[0:HOT, :] += spread[window:window + HOT, :]
    table_store = copy(spread.at[pl.ds(0, window)], table_out.at[0, 0], 4)
    act_load.wait()
    act_store = copy(act, act_out, 5)
    bottom_load.wait()
    bottom_store = copy(bottom, bottom_out, 6)
    act_store.wait()
    bottom_store.wait()
    table_store.wait()


def on_device(groups, shards, bottom_out, lookups, starts, tables, top_dense, top_pairs, cotangent):
    batch, width = bottom_out.shape
    hidden = cotangent.shape[1]
    bag = lookups.shape[2]
    window = tables.shape[1] // groups
    hot_rows = groups * HOT
    chips = shards // 2
    flipped = lookups[:, 0, :].T
    in_hbm = pl.BlockSpec(memory_space=pltpu.HBM)
    f32, bf16 = jnp.float32, jnp.bfloat16
    blocks = VMEM((chips, width, batch), f32)
    act, bottom_grad, hot_grad = pl.pallas_call(
        functools.partial(exchange_kernel, groups, shards, window),
        out_shape=(
            jax.ShapeDtypeStruct((batch, hidden), bf16),
            jax.ShapeDtypeStruct((batch, width), f32),
            jax.ShapeDtypeStruct((groups, HOT, width), f32),
        ),
        in_specs=[in_hbm] * 7,
        out_specs=(in_hbm, in_hbm, in_hbm),
        scratch_shapes=[
            pltpu.SMEM(starts.shape, jnp.int32),
            VMEM((batch, width), bf16),
            VMEM((width, hidden), bf16),
            VMEM((1, hidden), f32),
            VMEM((batch, hidden), f32),
            VMEM((groups, window + HOT, width), f32),
            VMEM((shards, bag, batch), jnp.int32),
            VMEM((shards, width, batch), f32),
            VMEM((hot_rows, shards * batch), bf16),
            VMEM((shards, width, batch), f32), blocks, blocks,
            VMEM((shards, 1, batch), f32),
            VMEM((2, shards, 1, batch), f32),
            VMEM((2 * width, shards * batch), bf16),
            VMEM((batch, hidden), f32),
            VMEM((batch, hidden), bf16),
            VMEM((batch, hidden), bf16),
            VMEM((batch, width), f32),
            VMEM((groups, HOT, width), f32),
            DMA((9,)), DMA((2 * groups,)),
            DMA((shards,)), DMA((shards,)), DMA((shards,)), DMA((shards,)),
            DMA((chips,)), DMA((chips,)), DMA((chips,)), DMA((chips,)),
            DMA((shards,)), DMA((shards,)), DMA((shards,)), DMA((shards,)),
            DMA((groups,)), DMA((groups,)),
        ],
        compiler_params=pltpu.CompilerParams(
            collective_id=0, has_side_effects=True, vmem_limit_bytes=VMEM_ALL
        ),
    )(starts, flipped, bottom_out, tables, top_dense, top_pairs, cotangent)
    return pl.pallas_call(
        functools.partial(place_kernel, groups, window),
        out_shape=(
            jax.ShapeDtypeStruct((batch, hidden), bf16),
            jax.ShapeDtypeStruct((batch, width), f32),
            jax.ShapeDtypeStruct((1, 1, window, width), f32),
        ),
        in_specs=[in_hbm] * 4,
        out_specs=(in_hbm, in_hbm, in_hbm),
        scratch_shapes=[
            VMEM((window + HOT, width), f32),
            pltpu.SMEM(starts.shape, jnp.int32),
            VMEM((groups, HOT, width), f32),
            VMEM((batch, hidden), bf16),
            VMEM((batch, width), f32),
            DMA((7,)),
        ],
        compiler_params=pltpu.CompilerParams(vmem_limit_bytes=VMEM_ALL),
    )(starts, hot_grad, act, bottom_grad)


def solution(mesh):
    groups, shards = mesh.shape["grp"], mesh.shape["shard"]
    in_specs = (
        P(("grp", "shard"), None),
        P(("grp", "shard"), None, None),
        P(),
        P(None, "shard", None),
        P(),
        P(),
        P(("grp", "shard"), None),
    )
    out_specs = (
        P(("grp", "shard"), None),
        P(("grp", "shard"), None),
        P(None, "shard", "grp", None),
    )
    return jax.shard_map(
        functools.partial(on_device, groups, shards),
        mesh=mesh, in_specs=in_specs, out_specs=out_specs, check_vma=False,
    )
```

time: 40.1 us -> 30 us (0.75)
  local copies, waits for them, and re-layouts: 6.93 us -> 0 us
  Pallas kernels: 32.2 us -> 29.2 us
    unnamed x14 -> x0, local copies, waits for them, and re-layouts: 6.93 us -> none
    pallas_call x1, Pallas kernels: 30.5 us -> 27.1 us  [on_device(): pl.pallas_call(functools.partial(exchange_kernel, groups, shards, window)...]
where the time goes in v2:
time: 30 us; the launch traced here: 29.8 us
  Pallas kernels  29.2 us (97%)
  between operations  0.64 us (2%)
    pallas_call x1, Pallas kernels, on_device(): pl.pallas_call(functools.partial(exchange_kernel, groups, shards, window)...  27.1 us
    pallas_call x1, Pallas kernels, on_device(): pl.pallas_call(functools.partial(place_kernel, groups, window), out_shape...  2.04 us

profile of v2, /device:TPU:0, one launch (start us, length us, event | category | flops | bytes accessed | tf_op | source)
XLA Modules:
  0.0 29.8 jit_solution(2695436027681493943)
XLA Ops:
  0.6 27.1 %shard_map.94 = (bf16[128,1024]{1,0:T(8,128)(2,1)}, f32[128,128]{1,0:T(8,128)}, f32[4,64,128]{2,1,0:T(8,128)}) custom-call(s32[4,32]{1,0:T(4,128)} %starts_ref.3, s32[4,128]{1,0:T(4,128)} %bitcast.3, bf16[128,128]{1,0:T(8,128)(2,1)} %bottom_ref.1, f32[1,7872,128]{2,1,0:T(8,128)} %tables_ref.1, bf16[128,1024]{1,0:T(8,128)(2,1)} %dense_ref.1, ...), custom_call_target="tpu_custom_call" | custom-call | tf_op jit(solution)/shard_map/pallas_call | solution.py:293
  27.8 2.0 %shard_map.95 = (bf16[128,1024]{1,0:T(8,128)(2,1)}, f32[128,128]{1,0:T(8,128)}, f32[1,1,1968,128]{3,2,1,0:T(8,128)}) custom-call(s32[4,32]{1,0:T(4,128)} %starts_ref.3, f32[4,64,128]{2,1,0:T(8,128)} %get-tuple-element.6.hot_ref, bf16[128,1024]{1,0:T(8,128)(2,1)} %get-tuple-element.7.act_in, f32[128,128]{1,0:T(8,128)} %get-tuple-element.8.bottom_in), custom_call_target="tpu_custom_call" | custom-call | tf_op jit(solution)/shard_map/pallas_call | solution.py:331

commit v3 on v2

--- a/solution.py
+++ b/solution.py
@@ -178,30 +178,24 @@
         remote(dots_all.at[peer], pair_all.at[0, peer], dots_send.at[peer], dots_recv.at[peer],
                shard=peer).wait_recv()
         dots = dots + pair_all[0, peer]
-    dots_col = jnp.broadcast_to(dots, (batch, batch)).T[:, 0:1]
+    dots_tile = jnp.broadcast_to(dots, (batch, batch)).T
 
     pairs_load.wait()
     cot_load.wait()
-    chunk = 256 if hidden % 256 == 0 else hidden
-    lanes = 128 if chunk % 128 == 0 else chunk
-    running = jnp.zeros((batch, lanes), jnp.float32)
-    for first in range(0, hidden, chunk):
-        cut = slice(first, first + chunk)
+    running = jnp.zeros((batch, batch), jnp.float32)
+    for first in range(0, hidden, batch):
+        cut = slice(first, first + batch)
         weights = pairs[0:1, cut]
-        preact = preact_ref[:, cut] + dots_col * weights
-        sig = jax.nn.sigmoid(preact)
-        preact_ref[:, cut] = preact * sig
+        preact = preact_ref[:, cut] + dots_tile * weights
+        sig = 0.5 + 0.5 * jnp.tanh(0.5 * preact)
+        act[:, cut] = (preact * sig).astype(jnp.bfloat16)
         pre_grad = cot[:, cut] * sig * (1.0 + preact * (1.0 - sig))
         half_ref[:, cut] = pre_grad.astype(jnp.bfloat16)
-        product = pre_grad * weights
-        for lane in range(0, chunk, lanes):
-            running = running + product[:, lane:lane + lanes]
-    pair_col = jnp.sum(running, axis=1, keepdims=True)
-    pair_all[1, me] = jnp.broadcast_to(pair_col, (batch, batch)).T[0:1]
+        running = running + pre_grad * weights
+    pair_all[1, me] = jnp.sum(running.T, axis=0, keepdims=True)
     for peer in peers:
         send(pair_all.at[1, me], pair_all.at[1, me], pair_send.at[peer], pair_recv.at[me], shard=peer)
 
-    act[...] = preact_ref[...].astype(jnp.bfloat16)
     act_store = load(act, act_ref, 6)
     bottom_dense = lax.dot_general(
         half_ref[...], dense[...], (((1,), (1,)), ((), ())), preferred_element_type=jnp.float32
@@ -213,19 +207,25 @@
         weighted[0:width, where] = high
         weighted[width:2 * width, where] = low
 
+    def pair_wait(source):
+        remote(pair_all.at[1, source], pair_all.at[1, source], pair_send.at[source], pair_recv.at[source],
+               shard=sib).wait_recv()
+
     weigh(me)
-    for peer in peers:
-        remote(pair_all.at[1, peer], pair_all.at[1, peer], pair_send.at[peer], pair_recv.at[peer],
-               shard=peer).wait_recv()
-        weigh(peer)
-    per_dot = 4 if groups % 4 == 0 else 1
-    for win in range(0, groups, per_dot):
-        both = lax.dot_general(
-            counts[win * HOT:(win + per_dot) * HOT, :], weighted[...],
-            (((1,), (1,)), ((), ())), preferred_element_type=jnp.float32)
-        summed = both[:, :width] + both[:, width:]
-        for step in range(per_dot):
-            grad_send[win + step] = summed[step * HOT:(step + 1) * HOT]
+    for other in [chip] + near_first:
+        if other is not chip:
+            pair_wait(other * 2 + core)
+            weigh(other * 2 + core)
+        pair_wait(other * 2 + 1 - core)
+        weigh(other * 2 + 1 - core)
+        where = pl.ds(pl.multiple_of(other * 2 * batch, batch), 2 * batch)
+        both = lax.dot_general(counts[:, where], weighted[:, where], (((1,), (1,)), ((), ())),
+                               preferred_element_type=jnp.float32)
+        summed = (both[:, :width] + both[:, width:]).reshape(groups, HOT, width)
+        if other is chip:
+            grad_send[...] = summed
+        else:
+            grad_send[...] = grad_send[...] + summed
     for peer in grp_peers:
         send(grad_send.at[peer], hot_out_ref.at[grp], grp_send.at[peer], grp_recv.at[grp], grp=peer)
     own_store = load(grad_send.at[grp], hot_out_ref.at[grp], 7)

time: 30 us -> 30.1 us (level)
  no operation moved by 1% of the time
where the time goes in v3:
time: 30.1 us; the launch traced here: 29.9 us
  Pallas kernels  29.3 us (97%)
  between operations  0.64 us (2%)
    pallas_call x1, Pallas kernels, on_device(): pl.pallas_call(functools.partial(exchange_kernel, groups, shards, window)...  27.2 us
    pallas_call x1, Pallas kernels, on_device(): pl.pallas_call(functools.partial(place_kernel, groups, window), out_shape...  2.04 us

profile of v3, /device:TPU:0, one launch (start us, length us, event | category | flops | bytes accessed | tf_op | source)
XLA Modules:
  0.0 29.9 jit_solution(9795966391637894581)
XLA Ops:
  0.6 27.2 %shard_map.94 = (bf16[128,1024]{1,0:T(8,128)(2,1)}, f32[128,128]{1,0:T(8,128)}, f32[4,64,128]{2,1,0:T(8,128)}) custom-call(s32[4,32]{1,0:T(4,128)} %starts_ref.3, s32[4,128]{1,0:T(4,128)} %bitcast.3, bf16[128,128]{1,0:T(8,128)(2,1)} %bottom_ref.1, f32[1,7872,128]{2,1,0:T(8,128)} %tables_ref.1, bf16[128,1024]{1,0:T(8,128)(2,1)} %dense_ref.1, ...), custom_call_target="tpu_custom_call" | custom-call | tf_op jit(solution)/shard_map/pallas_call | solution.py:293
  27.9 2.0 %shard_map.95 = (bf16[128,1024]{1,0:T(8,128)(2,1)}, f32[128,128]{1,0:T(8,128)}, f32[1,1,1968,128]{3,2,1,0:T(8,128)}) custom-call(s32[4,32]{1,0:T(4,128)} %starts_ref.3, f32[4,64,128]{2,1,0:T(8,128)} %get-tuple-element.6.hot_ref, bf16[128,1024]{1,0:T(8,128)(2,1)} %get-tuple-element.7.act_in, f32[128,128]{1,0:T(8,128)} %get-tuple-element.8.bottom_in), custom_call_target="tpu_custom_call" | custom-call | tf_op jit(solution)/shard_map/pallas_call | solution.py:331
